TPU v7x, 32 devices: a whole 2x2x4 slice. The times are simulated.
32 devices in a mesh: tm: 16 (over z, y, x), rows: 2 (over core).
Axes of the slice: x: 2, y: 2, z: 4, core: 2. Of those that a mesh axis runs over, the one named last changes fastest.
Arguments:
- resid: float32 [2, 16, 16, 512], P(None, 'tm', 'rows'), may hold values from -3 to 3
- basis: float32 [4, 2, 16, 16, 512], P(None, None, 'tm', 'rows'), may hold values from -0.01171875 to 0.01171875
Outputs:
- precond: float32 [2, 16, 16, 512], P(None, 'tm', 'rows')
- image: float32 [2, 16, 16, 512], P(None, 'tm', 'rows')
- gram: float32 [5], replicated
All inputs are finite; a program needn't handle non-finite values.
Results may differ from a plain program's by a relative error of at most 0.0005.
Values sent between devices are 32-bit elements; how exact they have to be, the bound alone decides.
A program may use at most 64 MiB of HBM per device.

v0:
```python
import math
import jax
import jax.numpy as jnp
from jax import lax
from jax.sharding import PartitionSpec as P

SWEEPS = 4
ALPHA = 0.01


def padded_2(shard, sides, width):
    for axis, dim in sides:
        count, length = (lax.axis_size(axis), shard.shape[dim])
        up = [(i, (i + 1) % count) for i in range(count - 1)]
        down = [(j, i) for i, j in up]
        last = lax.slice_in_dim(shard, length - width, length, axis=dim)
        first = lax.slice_in_dim(shard, 0, width, axis=dim)
        before = lax.ppermute(last, axis, up)
        after = lax.ppermute(first, axis, down)
        shard = jnp.concatenate([before, shard, after], axis=dim)
    return shard


def shifted(value, axis, steps):
    count = lax.axis_size(axis)
    first, last = (max(0, -steps), min(count, count - steps))
    return lax.ppermute(value, axis, [(source, source + steps) for source in range(first, last)])


def neighbours(padded):
    middle = padded[:, 1:-1]
    sides = jnp.pad(middle, ((0, 0), (0, 0), (1, 1)))
    return padded[:, 2:] + padded[:, :-2] + sides[:, :, 2:] + sides[:, :, :-2]


def cmul(left, right_re, right_im):
    return jnp.stack(
        [left[0] * right_re - left[1] * right_im, left[0] * right_im + left[1] * right_re]
    )


def phases(first, second, steps):
    turns = first * second % steps
    angle = turns.astype(jnp.float32) * (2.0 * math.pi / steps)
    return (jnp.cos(angle), jnp.sin(angle))


def on_device(resid, basis):
    steps = lax.axis_size("tm")
    coupling = 16.0 / (steps * steps)
    me = lax.axis_index("tm")
    rows_dev = resid.shape[2]
    cols = resid.shape[3]
    cells = rows_dev * cols
    piece = cells // steps
    mine = me.astype(jnp.float32)
    gamma = jnp.power(jnp.float32(ALPHA), mine / steps)
    scaled = resid[:, 0] * gamma
    ordinal = jnp.arange(steps, dtype=jnp.int32)
    cos_table, sin_table = phases(ordinal[:, None], ordinal[None, :], steps)
    blocks = lax.all_to_all(
        scaled.reshape(1, 2, cells), "tm", split_axis=2, concat_axis=0, tiled=True
    )
    flat = blocks.reshape(steps, 2 * piece)
    real_part = jnp.dot(cos_table, flat, precision=lax.Precision.HIGHEST)
    imag_part = -jnp.dot(sin_table, flat, precision=lax.Precision.HIGHEST)
    stacked = jnp.stack([real_part, imag_part], 1).reshape(steps, 2, 2, piece)
    spectrum = lax.all_to_all(stacked, "tm", split_axis=0, concat_axis=3, tiled=True)
    rhat = spectrum[0].reshape(2, 2, rows_dev, cols)
    base = jnp.power(jnp.float32(ALPHA), jnp.float32(1.0) / steps)
    angle = mine * (2.0 * math.pi / steps)
    lam_re = 1.0 - base * jnp.cos(angle)
    lam_im = base * jnp.sin(angle)
    disp_spec = rhat[:, 0]
    right = cmul(disp_spec, lam_re, lam_im) + rhat[:, 1]
    den_re = lam_re * lam_re - lam_im * lam_im + 4.0 * coupling
    den_im = 2.0 * lam_re * lam_im
    magnitude = den_re * den_re + den_im * den_im
    inv_re = den_re / magnitude
    inv_im = -den_im / magnitude
    uhat = cmul(right, inv_re, inv_im)
    for sweep in range(SWEEPS - 1):
        padded = padded_2(uhat, (("rows", 1),), 1)
        uhat = cmul(right + coupling * neighbours(padded), inv_re, inv_im)
    vhat = cmul(uhat, lam_re, lam_im) - disp_spec
    yhat = jnp.stack([uhat, vhat], 1)
    spread = lax.all_to_all(
        yhat.reshape(1, 2, 2, cells), "tm", split_axis=3, concat_axis=0, tiled=True
    )
    real_rows = spread[:, 0].reshape(steps, 2 * piece)
    imag_rows = spread[:, 1].reshape(steps, 2 * piece)
    undo = jnp.power(jnp.float32(ALPHA), -ordinal.astype(jnp.float32) / steps) / steps
    history = jnp.dot(cos_table, real_rows, precision=lax.Precision.HIGHEST) - jnp.dot(
        sin_table, imag_rows, precision=lax.Precision.HIGHEST
    )
    history = (history * undo[:, None]).reshape(steps, 2, piece)
    returned = lax.all_to_all(history, "tm", split_axis=0, concat_axis=2, tiled=True)
    precond = returned[0].reshape(2, rows_dev, cols)
    earlier = shifted(precond, "tm", 1)
    disp_rim = padded_2(precond[0:1], (("rows", 1),), 1)
    laplace = neighbours(disp_rim)[0] - 4.0 * precond[0]
    first = precond[0] - earlier[0] - precond[1]
    second = precond[1] - earlier[1] - coupling * laplace
    image = jnp.stack([first, second])
    inner = jnp.sum(basis[:, :, 0] * image[None], axis=(1, 2, 3))
    count = 2.0 * steps * rows_dev * lax.axis_size("rows") * cols
    squares = jnp.sum(image * image) / count
    local_terms = jnp.concatenate([inner, squares[None]])
    gram = lax.psum(local_terms, ("tm", "rows"))
    return (precond[:, None], image[:, None], gram)


def solution(mesh):
    in_specs = (P(None, "tm", "rows", None), P(None, None, "tm", "rows", None))
    out_specs = (P(None, "tm", "rows", None), P(None, "tm", "rows", None), P())
    return jax.shard_map(
        on_device, mesh=mesh, in_specs=in_specs, out_specs=out_specs, check_vma=False
    )
```

profile of v0, /device:TPU:0, one launch (start us, length us, event | category | flops | bytes accessed | tf_op | source)
XLA Modules:
  0.0 169.4 jit_solution(10434036143663607024)
XLA Ops:
  2.6 19.4 %reduce.4 = f32[4096,2]{1,0:T(8,128)} reduce(f32[4096,1,2]{2,1,0:T(1,128)S(1)} %bitcast.83, f32[]{:T(128)} %broadcast.139), dimensions={1}, to_apply=%bitcast.65.reduce_sub_computation | reduce | bytes 65540
  22.0 3.0 %reshape.138 = f32[16,1,512]{2,1,0:T(1,128)S(1)} reshape(f32[4096,2]{1,0:T(8,128)} %reduce.4) | data formatting | bytes 65536
  25.0 15.5 %all_to_all.63 = f32[16,1,512]{2,1,0:T(1,128)S(1)} all-to-all(f32[16,1,512]{2,1,0:T(1,128)S(1)} %reshape.138), channel_id=1, replica_groups=mesh['tm'=16,'rows'=2] {'tm'}, dimensions={0} | all-to-all | bytes 65536 | tf_op jit(solution)/shard_map/all_to_all | solution.py:61
  41.3 3.4 %reshape.139 = f32[4096,1,2]{2,1,0:T(1,128)S(1)} reshape(f32[16,512]{1,0:T(8,128)S(1)} %reduce.5) | data formatting | bytes 65536
  46.5 3.5 %all-to-all-start.1 = ((f32[16,2,2,256]{3,2,1,0:T(2,128)}), f32[16,2,2,256]{3,2,1,0:T(2,128)S(1)}, u32[]{:S(2)}, u32[]{:S(2)}) async-start(f32[16,2,2,256]{3,2,1,0:T(2,128)} %copy.48), calls=%async_computation.1 | async-start | bytes 131072 | tf_op jit(solution)/shard_map/all_to_all | solution.py:68
  50.2 7.2 %all-to-all-done.1 = f32[16,2,2,256]{3,2,1,0:T(2,128)S(1)} async-done(((f32[16,2,2,256]{3,2,1,0:T(2,128)}), f32[16,2,2,256]{3,2,1,0:T(2,128)S(1)}, u32[]{:S(2)}, u32[]{:S(2)}) %all-to-all-start.1) | async-done | bytes 65568 | tf_op jit(solution)/shard_map/all_to_all | solution.py:68
  57.6 1.3 collective-permute-start
  58.9 3.0 %collective-permute-start.1 = (f32[2,1,512]{2,1,0:T(1,128)S(1)}, f32[2,1,512]{2,1,0:T(1,128)S(1)}, u32[]{:S(2)}, u32[]{:S(2)}) collective-permute-start(f32[2,1,512]{2,1,0:T(1,128)S(1)} %get-tuple-element.26), channel_id=1, source_target_pairs={{0,1},{2,3},{4,5},{6,7},{8,9},{10,11},{12,13},{14,15},{16,17},{18,... | collective-permute-start | bytes 12296 | tf_op jit(solution)/shard_map/ppermute | solution.py:18
  62.9 1.3 collective-permute-start.2
  64.2 3.0 %collective-permute-start.3 = (f32[2,1,512]{2,1,0:T(1,128)S(1)}, f32[2,1,512]{2,1,0:T(1,128)S(1)}, u32[]{:S(2)}, u32[]{:S(2)}) collective-permute-start(f32[2,1,512]{2,1,0:T(1,128)S(1)} %get-tuple-element.22), channel_id=1, source_target_pairs={{0,1},{2,3},{4,5},{6,7},{8,9},{10,11},{12,13},{14,15},{16,17},{18,... | collective-permute-start | bytes 12296 | tf_op jit(solution)/shard_map/ppermute | solution.py:18
  68.1 1.3 collective-permute-start.4
  69.4 3.2 %collective-permute-start.5 = (f32[2,1,512]{2,1,0:T(1,128)S(1)}, f32[2,1,512]{2,1,0:T(1,128)S(1)}, u32[]{:S(2)}, u32[]{:S(2)}) collective-permute-start(f32[2,1,512]{2,1,0:T(1,128)S(1)} %get-tuple-element.18), channel_id=1, source_target_pairs={{0,1},{2,3},{4,5},{6,7},{8,9},{10,11},{12,13},{14,15},{16,17},{18,... | collective-permute-start | bytes 12296 | tf_op jit(solution)/shard_map/ppermute | solution.py:18
  73.5 4.4 %copy.51 = f32[1,2,2,4096]{2,1,0,3:T(2,128)} copy(f32[1,2,2,4096]{3,1,2,0:T(2,128)S(1)} %pad_maximum_fusion.1) | data formatting | bytes 131072 | tf_op jit(solution)/shard_map/stack | solution.py:86
  77.9 8.1 %reshape.140 = f32[16,1,1024]{2,1,0:T(1,128)} reshape(f32[4096,1,2,2]{3,2,1,0:T(2,128)} %bitcast.81) | data formatting | bytes 131072
  86.0 3.5 %all-to-all-start.2 = ((f32[16,1,1024]{2,1,0:T(1,128)}), f32[16,1,1024]{2,1,0:T(1,128)S(1)}, u32[]{:S(2)}, u32[]{:S(2)}) async-start(f32[16,1,1024]{2,1,0:T(1,128)} %reshape.140), calls=%async_computation.2 | async-start | bytes 131072 | tf_op jit(solution)/shard_map/all_to_all | solution.py:87
  89.5 7.5 %all-to-all-done.2 = f32[16,1,1024]{2,1,0:T(1,128)S(1)} async-done(((f32[16,1,1024]{2,1,0:T(1,128)}), f32[16,1,1024]{2,1,0:T(1,128)S(1)}, u32[]{:S(2)}, u32[]{:S(2)}) %all-to-all-start.2) | async-done | bytes 65568 | tf_op jit(solution)/shard_map/all_to_all | solution.py:87
  97.8 7.7 %reshape.141 = f32[4096,1,2,2]{3,2,1,0:T(2,128)} reshape(f32[16,1024]{1,0:T(8,128)S(1)} %reduce.6) | data formatting | bytes 131072
  105.6 3.6 %copy.57 = f32[1,2,2,16,256]{4,3,2,1,0:T(8,128)S(1)} copy(f32[1,2,2,16,256]{2,1,4,3,0:T(2,128)} %bitcast.82) | data formatting | bytes 131072 | tf_op jit(solution)/shard_map/all_to_all | solution.py:87
  109.7 10.0 %all_to_all.64 = f32[16,2,256]{2,1,0:T(2,128)S(1)} all-to-all(f32[16,2,256]{2,1,0:T(2,128)S(1)} %reshape.134), channel_id=1, replica_groups=mesh['tm'=16,'rows'=2] {'tm'}, dimensions={0} | all-to-all | bytes 65536 | tf_op jit(solution)/shard_map/all_to_all | solution.py:97
  119.8 2.6 %collective-permute-start.6 = (f32[2,8,512]{2,1,0:T(8,128)S(1)}, f32[2,8,512]{2,1,0:T(8,128)S(1)}, u32[]{:S(2)}, u32[]{:S(2)}) collective-permute-start(f32[2,8,512]{2,1,0:T(8,128)S(1)} %reshape_squeeze.15), channel_id=1, source_target_pairs={{0,2},{2,4},{4,6},{6,8},{8,10},{10,12},{12,14},{14,16},{16,18},{18... | collective-permute-start | bytes 98312 | tf_op jit(solution)/shard_map/ppermute | solution.py:27
  122.4 1.3 collective-permute-start.7
  123.7 3.0 %collective-permute-start.8 = (f32[1,1,512]{2,1,0:T(1,128)S(1)}, f32[1,1,512]{2,1,0:T(1,128)S(1)}, u32[]{:S(2)}, u32[]{:S(2)}) collective-permute-start(f32[1,1,512]{2,1,0:T(1,128)S(1)} %get-tuple-element.30), channel_id=1, source_target_pairs={{0,1},{2,3},{4,5},{6,7},{8,9},{10,11},{12,13},{14,15},{16,17},{18,... | collective-permute-start | bytes 6152 | tf_op jit(solution)/shard_map/ppermute | solution.py:18
  127.7 1.2 pad_maximum_fusion.18
  130.4 39.0 %psum.7 = f32[5]{0:T(128)} all-reduce(f32[5]{0:T(128)S(1)} %pad_maximum_fusion.21), channel_id=1, replica_groups=mesh['tm'=16,'rows'=2] {'tm','rows'}, use_global_device_ids=true, to_apply=%region_2.3 | all-reduce | flops 5 | bytes 40 | tf_op jit(solution)/shard_map/psum | solution.py:109
  (66 shorter events, 10.2 us)
Async XLA Ops:
  46.5 11.0 %all-to-all-start.1 = ((f32[16,2,2,256]{3,2,1,0:T(2,128)}), f32[16,2,2,256]{3,2,1,0:T(2,128)S(1)}, u32[]{:S(2)}, u32[]{:S(2)}) async-start(f32[16,2,2,256]{3,2,1,0:T(2,128)} %copy.48), calls=%async_computation.1 | async-start | bytes 131072 | tf_op jit(solution)/shard_map/all_to_all | solution.py:68
  57.6 4.3 %collective-permute-start = (f32[2,1,512]{2,1,0:T(1,128)S(1)}, f32[2,1,512]{2,1,0:T(1,128)S(1)}, u32[]{:S(2)}, u32[]{:S(2)}) collective-permute-start(f32[2,1,512]{2,1,0:T(1,128)S(1)} %get-tuple-element.25), channel_id=1, source_target_pairs={{1,0},{3,2},{5,4},{7,6},{9,8},{11,10},{13,12},{15,14},{17,16},{19,... | collective-permute-start | bytes 12296 | tf_op jit(solution)/shard_map/ppermute | solution.py:19
  58.9 3.8 %collective-permute-start.1 = (f32[2,1,512]{2,1,0:T(1,128)S(1)}, f32[2,1,512]{2,1,0:T(1,128)S(1)}, u32[]{:S(2)}, u32[]{:S(2)}) collective-permute-start(f32[2,1,512]{2,1,0:T(1,128)S(1)} %get-tuple-element.26), channel_id=1, source_target_pairs={{0,1},{2,3},{4,5},{6,7},{8,9},{10,11},{12,13},{14,15},{16,17},{18,... | collective-permute-start | bytes 12296 | tf_op jit(solution)/shard_map/ppermute | solution.py:18
  62.9 4.3 %collective-permute-start.2 = (f32[2,1,512]{2,1,0:T(1,128)S(1)}, f32[2,1,512]{2,1,0:T(1,128)S(1)}, u32[]{:S(2)}, u32[]{:S(2)}) collective-permute-start(f32[2,1,512]{2,1,0:T(1,128)S(1)} %get-tuple-element.21), channel_id=1, source_target_pairs={{1,0},{3,2},{5,4},{7,6},{9,8},{11,10},{13,12},{15,14},{17,16},{19,... | collective-permute-start | bytes 12296 | tf_op jit(solution)/shard_map/ppermute | solution.py:19
  64.2 3.8 %collective-permute-start.3 = (f32[2,1,512]{2,1,0:T(1,128)S(1)}, f32[2,1,512]{2,1,0:T(1,128)S(1)}, u32[]{:S(2)}, u32[]{:S(2)}) collective-permute-start(f32[2,1,512]{2,1,0:T(1,128)S(1)} %get-tuple-element.22), channel_id=1, source_target_pairs={{0,1},{2,3},{4,5},{6,7},{8,9},{10,11},{12,13},{14,15},{16,17},{18,... | collective-permute-start | bytes 12296 | tf_op jit(solution)/shard_map/ppermute | solution.py:18
  68.1 4.5 %collective-permute-start.4 = (f32[2,1,512]{2,1,0:T(1,128)S(1)}, f32[2,1,512]{2,1,0:T(1,128)S(1)}, u32[]{:S(2)}, u32[]{:S(2)}) collective-permute-start(f32[2,1,512]{2,1,0:T(1,128)S(1)} %get-tuple-element.17), channel_id=1, source_target_pairs={{1,0},{3,2},{5,4},{7,6},{9,8},{11,10},{13,12},{15,14},{17,16},{19,... | collective-permute-start | bytes 12296 | tf_op jit(solution)/shard_map/ppermute | solution.py:19
  69.4 3.8 %collective-permute-start.5 = (f32[2,1,512]{2,1,0:T(1,128)S(1)}, f32[2,1,512]{2,1,0:T(1,128)S(1)}, u32[]{:S(2)}, u32[]{:S(2)}) collective-permute-start(f32[2,1,512]{2,1,0:T(1,128)S(1)} %get-tuple-element.18), channel_id=1, source_target_pairs={{0,1},{2,3},{4,5},{6,7},{8,9},{10,11},{12,13},{14,15},{16,17},{18,... | collective-permute-start | bytes 12296 | tf_op jit(solution)/shard_map/ppermute | solution.py:18
  86.0 11.0 %all-to-all-start.2 = ((f32[16,1,1024]{2,1,0:T(1,128)}), f32[16,1,1024]{2,1,0:T(1,128)S(1)}, u32[]{:S(2)}, u32[]{:S(2)}) async-start(f32[16,1,1024]{2,1,0:T(1,128)} %reshape.140), calls=%async_computation.2 | async-start | bytes 131072 | tf_op jit(solution)/shard_map/all_to_all | solution.py:87
  105.6 24.0 %copy-start = (f32[4,2,1,8,512]{4,3,2,1,0:T(8,128)S(1)}, f32[4,2,1,8,512]{4,3,2,1,0:T(8,128)}, u32[]{:S(2)}) copy-start(f32[4,2,1,8,512]{4,3,2,1,0:T(8,128)} %param.3) | copy-start | bytes 393220
  119.8 7.8 %collective-permute-start.6 = (f32[2,8,512]{2,1,0:T(8,128)S(1)}, f32[2,8,512]{2,1,0:T(8,128)S(1)}, u32[]{:S(2)}, u32[]{:S(2)}) collective-permute-start(f32[2,8,512]{2,1,0:T(8,128)S(1)} %reshape_squeeze.15), channel_id=1, source_target_pairs={{0,2},{2,4},{4,6},{6,8},{8,10},{10,12},{12,14},{14,16},{16,18},{18... | collective-permute-start | bytes 98312 | tf_op jit(solution)/shard_map/ppermute | solution.py:27
  122.4 4.4 %collective-permute-start.7 = (f32[1,1,512]{2,1,0:T(1,128)S(1)}, f32[1,1,512]{2,1,0:T(1,128)S(1)}, u32[]{:S(2)}, u32[]{:S(2)}) collective-permute-start(f32[1,1,512]{2,1,0:T(1,128)S(1)} %get-tuple-element.29), channel_id=1, source_target_pairs={{1,0},{3,2},{5,4},{7,6},{9,8},{11,10},{13,12},{15,14},{17,16},{19,... | collective-permute-start | bytes 6152 | tf_op jit(solution)/shard_map/ppermute | solution.py:19
  123.7 3.8 %collective-permute-start.8 = (f32[1,1,512]{2,1,0:T(1,128)S(1)}, f32[1,1,512]{2,1,0:T(1,128)S(1)}, u32[]{:S(2)}, u32[]{:S(2)}) collective-permute-start(f32[1,1,512]{2,1,0:T(1,128)S(1)} %get-tuple-element.30), channel_id=1, source_target_pairs={{0,1},{2,3},{4,5},{6,7},{8,9},{10,11},{12,13},{14,15},{16,17},{18,... | collective-permute-start | bytes 6152 | tf_op jit(solution)/shard_map/ppermute | solution.py:18
where the time goes:
time: 170 us; the launch traced here: 169 us
  blocking collectives  64.5 us (38%)
  local copies, waits for them, and re-layouts  33.7 us (20%)
  starting transfers between devices  27 us (16%)
  other arithmetic  23.6 us (14%)
  waiting for transfers between devices  17.7 us (10%)
  between operations  2.06 us (1%)
    psum x1, blocking collectives, on_device(): gram = lax.psum(local_terms, ('tm', 'rows'))  39 us
    unnamed x10, local copies, waits for them, and re-layouts  22.8 us
    unnamed x1, other arithmetic  19.4 us
    all_to_all x1, blocking collectives, on_device(): lax.all_to_all(scaled.reshape(1, 2, cells), 'tm', split_axis=2, concat_ax...  15.5 us
    ppermute x4, starting transfers between devices, padded_2(): before = lax.ppermute(last, axis, up)  12.3 us
    all_to_all x1, blocking collectives, on_device(): lax.all_to_all(history, 'tm', split_axis=0, concat_axis=2, tiled=True)  9.98 us
    all_to_all x1, waiting for transfers between devices, on_device(): lax.all_to_all(yhat.reshape(1, 2, 2, cells), 'tm', split_axis=3, concat_a...  7.49 us
    all_to_all x1, waiting for transfers between devices, on_device(): lax.all_to_all(stacked, 'tm', split_axis=0, concat_axis=3, tiled=True)  7.25 us
  transfers between devices with their start and end apart: 11, of which 6 were waited for; matrix products, arithmetic and copies ran while one was open for 0% of the time, Pallas kernels for 0%

commit v1 on v0

--- a/solution.py
+++ b/solution.py
@@ -106,7 +106,7 @@
     count = 2.0 * steps * rows_dev * lax.axis_size("rows") * cols
     squares = jnp.sum(image * image) / count
     local_terms = jnp.concatenate([inner, squares[None]])
-    gram = lax.psum(local_terms, ("tm", "rows"))
+    gram = jnp.sum(lax.all_gather(local_terms, ("tm", "rows")), axis=0)
     return (precond[:, None], image[:, None], gram)
 
 

time: 170 us -> 170 us (level)
    unnamed x0 -> x1, blocking collectives: none -> 39 us
    psum x1 -> x0, blocking collectives: 39 us -> none  [on_device(): gram = lax.psum(local_terms, ('tm', 'rows'))]
    unnamed x1 -> x2, other arithmetic: 19.4 us -> 19.5 us
    unnamed x10 -> x11, local copies, waits for them, and re-layouts: 22.8 us -> 22.8 us
where the time goes in v1:
time: 170 us
  blocking collectives  64.6 us (38%)
  local copies, waits for them, and re-layouts  33.8 us (20%)
  starting transfers between devices  27 us (16%)
  other arithmetic  24.2 us (14%)
  waiting for transfers between devices  17.1 us (10%)
  between operations  2.02 us (1%)
    unnamed x1, blocking collectives  39 us
    unnamed x11, local copies, waits for them, and re-layouts  22.8 us
    unnamed x2, other arithmetic  19.5 us
    all_to_all x1, blocking collectives, on_device(): lax.all_to_all(scaled.reshape(1, 2, cells), 'tm', split_axis=2, concat_ax...  15.5 us
    ppermute x4, starting transfers between devices, padded_2(): before = lax.ppermute(last, axis, up)  12.3 us
    all_to_all x1, blocking collectives, on_device(): lax.all_to_all(history, 'tm', split_axis=0, concat_axis=2, tiled=True)  9.98 us
    all_to_all x1, waiting for transfers between devices, on_device(): lax.all_to_all(yhat.reshape(1, 2, 2, cells), 'tm', split_axis=3, concat_a...  7.49 us
    all_to_all x1, waiting for transfers between devices, on_device(): lax.all_to_all(stacked, 'tm', split_axis=0, concat_axis=3, tiled=True)  7.25 us
  transfers between devices with their start and end apart: 11, of which 6 were waited for; matrix products, arithmetic and copies ran while one was open for 0% of the time, Pallas kernels for 0%

profile of v1, /device:TPU:0, one launch (start us, length us, event | category | flops | bytes accessed | tf_op | source)
XLA Modules:
  0.0 169.5 jit_solution(8464165860491672188)
XLA Ops:
  2.6 19.4 %reduce.4 = f32[4096,2]{1,0:T(8,128)} reduce(f32[4096,1,2]{2,1,0:T(1,128)S(1)} %bitcast.83, f32[]{:T(128)} %broadcast.140), dimensions={1}, to_apply=%bitcast.65.reduce_sub_computation | reduce | bytes 65540
  22.0 3.0 %reshape.141 = f32[16,1,512]{2,1,0:T(1,128)S(1)} reshape(f32[4096,2]{1,0:T(8,128)} %reduce.4) | data formatting | bytes 65536
  25.0 15.5 %all_to_all.63 = f32[16,1,512]{2,1,0:T(1,128)S(1)} all-to-all(f32[16,1,512]{2,1,0:T(1,128)S(1)} %reshape.141), channel_id=1, replica_groups=mesh['tm'=16,'rows'=2] {'tm'}, dimensions={0} | all-to-all | bytes 65536 | tf_op jit(solution)/shard_map/all_to_all | solution.py:61
  41.3 3.4 %reshape.142 = f32[4096,1,2]{2,1,0:T(1,128)S(1)} reshape(f32[16,512]{1,0:T(8,128)S(1)} %reduce.5) | data formatting | bytes 65536
  46.5 3.5 %all-to-all-start.1 = ((f32[16,2,2,256]{3,2,1,0:T(2,128)}), f32[16,2,2,256]{3,2,1,0:T(2,128)S(1)}, u32[]{:S(2)}, u32[]{:S(2)}) async-start(f32[16,2,2,256]{3,2,1,0:T(2,128)} %copy.48), calls=%async_computation.1 | async-start | bytes 131072 | tf_op jit(solution)/shard_map/all_to_all | solution.py:68
  50.3 7.2 %all-to-all-done.1 = f32[16,2,2,256]{3,2,1,0:T(2,128)S(1)} async-done(((f32[16,2,2,256]{3,2,1,0:T(2,128)}), f32[16,2,2,256]{3,2,1,0:T(2,128)S(1)}, u32[]{:S(2)}, u32[]{:S(2)}) %all-to-all-start.1) | async-done | bytes 65568 | tf_op jit(solution)/shard_map/all_to_all | solution.py:68
  57.6 1.3 collective-permute-start
  58.9 3.0 %collective-permute-start.1 = (f32[2,1,512]{2,1,0:T(1,128)S(1)}, f32[2,1,512]{2,1,0:T(1,128)S(1)}, u32[]{:S(2)}, u32[]{:S(2)}) collective-permute-start(f32[2,1,512]{2,1,0:T(1,128)S(1)} %get-tuple-element.26), channel_id=1, source_target_pairs={{0,1},{2,3},{4,5},{6,7},{8,9},{10,11},{12,13},{14,15},{16,17},{18,... | collective-permute-start | bytes 12296 | tf_op jit(solution)/shard_map/ppermute | solution.py:18
  62.9 1.3 collective-permute-start.2
  64.2 3.0 %collective-permute-start.3 = (f32[2,1,512]{2,1,0:T(1,128)S(1)}, f32[2,1,512]{2,1,0:T(1,128)S(1)}, u32[]{:S(2)}, u32[]{:S(2)}) collective-permute-start(f32[2,1,512]{2,1,0:T(1,128)S(1)} %get-tuple-element.22), channel_id=1, source_target_pairs={{0,1},{2,3},{4,5},{6,7},{8,9},{10,11},{12,13},{14,15},{16,17},{18,... | collective-permute-start | bytes 12296 | tf_op jit(solution)/shard_map/ppermute | solution.py:18
  68.1 1.3 collective-permute-start.4
  69.4 3.2 %collective-permute-start.5 = (f32[2,1,512]{2,1,0:T(1,128)S(1)}, f32[2,1,512]{2,1,0:T(1,128)S(1)}, u32[]{:S(2)}, u32[]{:S(2)}) collective-permute-start(f32[2,1,512]{2,1,0:T(1,128)S(1)} %get-tuple-element.18), channel_id=1, source_target_pairs={{0,1},{2,3},{4,5},{6,7},{8,9},{10,11},{12,13},{14,15},{16,17},{18,... | collective-permute-start | bytes 12296 | tf_op jit(solution)/shard_map/ppermute | solution.py:18
  73.5 4.4 %copy.51 = f32[1,2,2,4096]{2,1,0,3:T(2,128)} copy(f32[1,2,2,4096]{3,1,2,0:T(2,128)S(1)} %pad_maximum_fusion.1) | data formatting | bytes 131072 | tf_op jit(solution)/shard_map/stack | solution.py:86
  77.9 8.1 %reshape.143 = f32[16,1,1024]{2,1,0:T(1,128)} reshape(f32[4096,1,2,2]{3,2,1,0:T(2,128)} %bitcast.81) | data formatting | bytes 131072
  86.0 3.5 %all-to-all-start.2 = ((f32[16,1,1024]{2,1,0:T(1,128)}), f32[16,1,1024]{2,1,0:T(1,128)S(1)}, u32[]{:S(2)}, u32[]{:S(2)}) async-start(f32[16,1,1024]{2,1,0:T(1,128)} %reshape.143), calls=%async_computation.2 | async-start | bytes 131072 | tf_op jit(solution)/shard_map/all_to_all | solution.py:87
  89.5 7.5 %all-to-all-done.2 = f32[16,1,1024]{2,1,0:T(1,128)S(1)} async-done(((f32[16,1,1024]{2,1,0:T(1,128)}), f32[16,1,1024]{2,1,0:T(1,128)S(1)}, u32[]{:S(2)}, u32[]{:S(2)}) %all-to-all-start.2) | async-done | bytes 65568 | tf_op jit(solution)/shard_map/all_to_all | solution.py:87
  97.8 7.7 %reshape.144 = f32[4096,1,2,2]{3,2,1,0:T(2,128)} reshape(f32[16,1024]{1,0:T(8,128)S(1)} %reduce.6) | data formatting | bytes 131072
  105.6 3.6 %copy.57 = f32[1,2,2,16,256]{4,3,2,1,0:T(8,128)S(1)} copy(f32[1,2,2,16,256]{2,1,4,3,0:T(2,128)} %bitcast.82) | data formatting | bytes 131072 | tf_op jit(solution)/shard_map/all_to_all | solution.py:87
  109.7 10.0 %all_to_all.64 = f32[16,2,256]{2,1,0:T(2,128)S(1)} all-to-all(f32[16,2,256]{2,1,0:T(2,128)S(1)} %reshape.134), channel_id=1, replica_groups=mesh['tm'=16,'rows'=2] {'tm'}, dimensions={0} | all-to-all | bytes 65536 | tf_op jit(solution)/shard_map/all_to_all | solution.py:97
  119.8 2.6 %collective-permute-start.6 = (f32[2,8,512]{2,1,0:T(8,128)S(1)}, f32[2,8,512]{2,1,0:T(8,128)S(1)}, u32[]{:S(2)}, u32[]{:S(2)}) collective-permute-start(f32[2,8,512]{2,1,0:T(8,128)S(1)} %reshape_squeeze.15), channel_id=1, source_target_pairs={{0,2},{2,4},{4,6},{6,8},{8,10},{10,12},{12,14},{14,16},{16,18},{18... | collective-permute-start | bytes 98312 | tf_op jit(solution)/shard_map/ppermute | solution.py:27
  122.5 1.3 collective-permute-start.7
  123.8 3.0 %collective-permute-start.8 = (f32[1,1,512]{2,1,0:T(1,128)S(1)}, f32[1,1,512]{2,1,0:T(1,128)S(1)}, u32[]{:S(2)}, u32[]{:S(2)}) collective-permute-start(f32[1,1,512]{2,1,0:T(1,128)S(1)} %get-tuple-element.30), channel_id=1, source_target_pairs={{0,1},{2,3},{4,5},{6,7},{8,9},{10,11},{12,13},{14,15},{16,17},{18,... | collective-permute-start | bytes 6152 | tf_op jit(solution)/shard_map/ppermute | solution.py:18
  127.7 1.2 pad_maximum_fusion.18
  129.9 39.0 %all-reduce.4 = f32[160]{0:T(256)S(1)} all-reduce(f32[160]{0:T(256)S(1)} %maximum_dynamic-update-slice_fusion), channel_id=2, replica_groups=mesh['tm'=16,'rows'=2] {'tm','rows'}, use_global_device_ids=true, to_apply=%add.4 | all-reduce | flops 160 | bytes 1280
  (69 shorter events, 10.3 us)
Async XLA Ops:
  46.5 11.0 %all-to-all-start.1 = ((f32[16,2,2,256]{3,2,1,0:T(2,128)}), f32[16,2,2,256]{3,2,1,0:T(2,128)S(1)}, u32[]{:S(2)}, u32[]{:S(2)}) async-start(f32[16,2,2,256]{3,2,1,0:T(2,128)} %copy.48), calls=%async_computation.1 | async-start | bytes 131072 | tf_op jit(solution)/shard_map/all_to_all | solution.py:68
  57.6 4.3 %collective-permute-start = (f32[2,1,512]{2,1,0:T(1,128)S(1)}, f32[2,1,512]{2,1,0:T(1,128)S(1)}, u32[]{:S(2)}, u32[]{:S(2)}) collective-permute-start(f32[2,1,512]{2,1,0:T(1,128)S(1)} %get-tuple-element.25), channel_id=1, source_target_pairs={{1,0},{3,2},{5,4},{7,6},{9,8},{11,10},{13,12},{15,14},{17,16},{19,... | collective-permute-start | bytes 12296 | tf_op jit(solution)/shard_map/ppermute | solution.py:19
  58.9 3.8 %collective-permute-start.1 = (f32[2,1,512]{2,1,0:T(1,128)S(1)}, f32[2,1,512]{2,1,0:T(1,128)S(1)}, u32[]{:S(2)}, u32[]{:S(2)}) collective-permute-start(f32[2,1,512]{2,1,0:T(1,128)S(1)} %get-tuple-element.26), channel_id=1, source_target_pairs={{0,1},{2,3},{4,5},{6,7},{8,9},{10,11},{12,13},{14,15},{16,17},{18,... | collective-permute-start | bytes 12296 | tf_op jit(solution)/shard_map/ppermute | solution.py:18
  62.9 4.3 %collective-permute-start.2 = (f32[2,1,512]{2,1,0:T(1,128)S(1)}, f32[2,1,512]{2,1,0:T(1,128)S(1)}, u32[]{:S(2)}, u32[]{:S(2)}) collective-permute-start(f32[2,1,512]{2,1,0:T(1,128)S(1)} %get-tuple-element.21), channel_id=1, source_target_pairs={{1,0},{3,2},{5,4},{7,6},{9,8},{11,10},{13,12},{15,14},{17,16},{19,... | collective-permute-start | bytes 12296 | tf_op jit(solution)/shard_map/ppermute | solution.py:19
  64.2 3.8 %collective-permute-start.3 = (f32[2,1,512]{2,1,0:T(1,128)S(1)}, f32[2,1,512]{2,1,0:T(1,128)S(1)}, u32[]{:S(2)}, u32[]{:S(2)}) collective-permute-start(f32[2,1,512]{2,1,0:T(1,128)S(1)} %get-tuple-element.22), channel_id=1, source_target_pairs={{0,1},{2,3},{4,5},{6,7},{8,9},{10,11},{12,13},{14,15},{16,17},{18,... | collective-permute-start | bytes 12296 | tf_op jit(solution)/shard_map/ppermute | solution.py:18
  68.1 4.5 %collective-permute-start.4 = (f32[2,1,512]{2,1,0:T(1,128)S(1)}, f32[2,1,512]{2,1,0:T(1,128)S(1)}, u32[]{:S(2)}, u32[]{:S(2)}) collective-permute-start(f32[2,1,512]{2,1,0:T(1,128)S(1)} %get-tuple-element.17), channel_id=1, source_target_pairs={{1,0},{3,2},{5,4},{7,6},{9,8},{11,10},{13,12},{15,14},{17,16},{19,... | collective-permute-start | bytes 12296 | tf_op jit(solution)/shard_map/ppermute | solution.py:19
  69.4 3.8 %collective-permute-start.5 = (f32[2,1,512]{2,1,0:T(1,128)S(1)}, f32[2,1,512]{2,1,0:T(1,128)S(1)}, u32[]{:S(2)}, u32[]{:S(2)}) collective-permute-start(f32[2,1,512]{2,1,0:T(1,128)S(1)} %get-tuple-element.18), channel_id=1, source_target_pairs={{0,1},{2,3},{4,5},{6,7},{8,9},{10,11},{12,13},{14,15},{16,17},{18,... | collective-permute-start | bytes 12296 | tf_op jit(solution)/shard_map/ppermute | solution.py:18
  86.0 11.0 %all-to-all-start.2 = ((f32[16,1,1024]{2,1,0:T(1,128)}), f32[16,1,1024]{2,1,0:T(1,128)S(1)}, u32[]{:S(2)}, u32[]{:S(2)}) async-start(f32[16,1,1024]{2,1,0:T(1,128)} %reshape.143), calls=%async_computation.2 | async-start | bytes 131072 | tf_op jit(solution)/shard_map/all_to_all | solution.py:87
  105.6 24.0 %copy-start = (f32[4,2,1,8,512]{4,3,2,1,0:T(8,128)S(1)}, f32[4,2,1,8,512]{4,3,2,1,0:T(8,128)}, u32[]{:S(2)}) copy-start(f32[4,2,1,8,512]{4,3,2,1,0:T(8,128)} %param.3) | copy-start | bytes 393220
  119.8 7.8 %collective-permute-start.6 = (f32[2,8,512]{2,1,0:T(8,128)S(1)}, f32[2,8,512]{2,1,0:T(8,128)S(1)}, u32[]{:S(2)}, u32[]{:S(2)}) collective-permute-start(f32[2,8,512]{2,1,0:T(8,128)S(1)} %reshape_squeeze.15), channel_id=1, source_target_pairs={{0,2},{2,4},{4,6},{6,8},{8,10},{10,12},{12,14},{14,16},{16,18},{18... | collective-permute-start | bytes 98312 | tf_op jit(solution)/shard_map/ppermute | solution.py:27
  122.5 5.0 %collective-permute-start.7 = (f32[1,1,512]{2,1,0:T(1,128)S(1)}, f32[1,1,512]{2,1,0:T(1,128)S(1)}, u32[]{:S(2)}, u32[]{:S(2)}) collective-permute-start(f32[1,1,512]{2,1,0:T(1,128)S(1)} %get-tuple-element.29), channel_id=1, source_target_pairs={{1,0},{3,2},{5,4},{7,6},{9,8},{11,10},{13,12},{15,14},{17,16},{19,... | collective-permute-start | bytes 6152 | tf_op jit(solution)/shard_map/ppermute | solution.py:19
  123.8 3.8 %collective-permute-start.8 = (f32[1,1,512]{2,1,0:T(1,128)S(1)}, f32[1,1,512]{2,1,0:T(1,128)S(1)}, u32[]{:S(2)}, u32[]{:S(2)}) collective-permute-start(f32[1,1,512]{2,1,0:T(1,128)S(1)} %get-tuple-element.30), channel_id=1, source_target_pairs={{0,1},{2,3},{4,5},{6,7},{8,9},{10,11},{12,13},{14,15},{16,17},{18,... | collective-permute-start | bytes 6152 | tf_op jit(solution)/shard_map/ppermute | solution.py:18
